TPU v7x, 512 devices: a whole 4x8x8 slice. The times are simulated.
512 devices in a mesh: replica: 16 (over z, core), mp: 16 (over y, x_hi), refresh: 2 (over x_lo).
Axes of the slice: x: 4 (x_hi: 2, x_lo: 2; x = x_hi * 2 + x_lo), y: 8, z: 8, core: 2. Of those that a mesh axis runs over, the one named last changes fastest.
Arguments:
- grad_partial: bfloat16 [16, 2, 512, 8192], P('replica', 'refresh', 'mp'), may hold values from -63 to 63
- left_stats: float32 [2, 512, 8192], P('refresh', 'replica', 'mp'), may hold values from -4608 to 5120, as said below
- right_stats: float32 [2, 512, 8192], P('refresh', 'replica', 'mp'), may hold values from -4608 to 5120, as said below
- left_roots: float32 [2, 512, 8192], P('refresh', 'replica', 'mp'), may hold values from -1 to 1, as said below
- right_roots: float32 [2, 512, 8192], P('refresh', 'replica', 'mp'), may hold values from -1 to 1, as said below
- newton_counts: int32 [2, 16], replicated, may hold values from 1 to 4
- owner: int32 [2, 16], replicated, may hold values from 0 to 15, each once within a row
Outputs:
- update: float32 [2, 512, 8192], P('refresh', 'mp')
- new_left_stats: float32 [2, 512, 8192], P('refresh', 'replica', 'mp')
- new_right_stats: float32 [2, 512, 8192], P('refresh', 'replica', 'mp')
- new_left_roots: float32 [2, 512, 8192], P('refresh', 'replica', 'mp')
- new_right_roots: float32 [2, 512, 8192], P('refresh', 'replica', 'mp')
Inputs may be any that keep to these rules, and one draw needn't show every extreme that they name: Each row of owner names every owner index once. `left_stats`: every 512 x 512 block is symmetric positive definite. `right_stats`: every 512 x 512 block is symmetric positive definite. `left_roots`: every 512 x 512 block is symmetric. `right_roots`: every 512 x 512 block is symmetric.
All inputs are finite; a program needn't handle non-finite values.
Results may differ from a plain program's by a relative error of at most 0.0003.
Values may be sent and summed in bfloat16 or wider, within the bound.
No kernel may reach another device: no remote copies, remote signals or barrier semaphores. Data moves between devices by JAX's collectives and lax.ppermute only.
A program may use at most 64 MiB of HBM per device.

v0:
```python
import functools

import jax
import jax.numpy as jnp
from jax import lax
from jax.sharding import Mesh
from jax.sharding import PartitionSpec as P

MP = ("mp_0", "mp_1")
REPLICA = ("replica_0", "replica_1")
REPLICA_MP_REFRESH = ("replica_0", "replica_1", "mp_0", "mp_1", "refresh")


decay = 0.9
graft_eps = 1e-06


def split_up(shard, dim, count):
    before, after = (shard.shape[:dim], shard.shape[dim + 1 :])
    return jnp.moveaxis(shard.reshape(*before, count, -1, *after), dim, 0)


def summed_on_arrival(shard, axis, dim):
    tiles = split_up(shard, dim, lax.axis_size(axis))
    arrived = lax.all_to_all(tiles, axis, split_axis=0, concat_axis=0, tiled=True)
    return arrived.sum(axis=0)


def by_axis(shard, axes):
    return functools.reduce(lax.psum, axes, shard)


def side_by_side(arrays, axis, dim, along):
    widths = [a.shape[along] for a in arrays]
    both = jnp.concatenate(arrays, axis=along)
    filled = lax.all_gather(both, axis, axis=dim, tiled=True)
    return tuple(jnp.split(filled, [sum(widths[:k]) for k in range(1, len(widths))], axis=along))


def swapped(shard, axis, stride):
    return lax.ppermute(shard, axis, [(i, i ^ 1 << stride) for i in range(lax.axis_size(axis))])


def sent_to_all(shard, axis):
    count = lax.axis_size(axis)
    return lax.all_to_all(
        jnp.broadcast_to(shard[None], (count, *shard.shape)), axis, 0, 0, tiled=True
    )


def laid_out(tiles, dim):
    lengths = list(tiles.shape[1:])
    lengths[dim] *= tiles.shape[0]
    return jnp.moveaxis(tiles, 0, dim).reshape(lengths)


def gather_directly(shard, axis, dim):
    tiles = sent_to_all(shard, axis)
    return laid_out(tiles, dim)


def product(left, right):
    return jnp.dot(left, right, precision=lax.Precision.HIGHEST, preferred_element_type=jnp.float32)


def newton_step(iterate, coupled, coupled_full, eye):
    factor = (5.0 * eye - coupled_full) * 0.25
    next_iterate = product(iterate, factor)
    next_coupled = product(product(product(product(coupled, factor), factor), factor), factor)
    return (next_iterate, next_coupled)


def run_iterations(advance, state, count):
    return lax.fori_loop(0, count, advance, state)


def make_folder(grad_rows, left_slab, replica_index, rows_rep):

    def fold_rows(carry, piece, start):
        left_acc = product(grad_rows, piece.T)
        own_cols = lax.dynamic_slice_in_dim(piece, replica_index * rows_rep, rows_rep, 1)
        right_acc = product(own_cols.T, piece)
        half_acc = product(left_slab, piece)
        return (left_acc, right_acc, half_acc)

    return fold_rows


def local(grad_partial, left_stats, right_stats, left_roots, right_roots, newton_counts, owner):
    group = lax.axis_index("refresh")
    owner_index = lax.axis_index(MP)
    replica_index = lax.axis_index(REPLICA)
    owners = lax.axis_size(MP)
    replicas = lax.axis_size(REPLICA)
    rows_part = grad_partial[0, 0]
    rows_mp = rows_part.shape[0]
    order = rows_part.shape[1] // owners
    rows_rep = order // replicas
    owner_row = lax.dynamic_index_in_dim(owner, group, 0, keepdims=False)
    counts_row = lax.dynamic_index_in_dim(newton_counts, group, 0, keepdims=False)
    slots = jnp.arange(owners, dtype=jnp.int32)
    hits = owner_row[:, None] == slots[None, :]
    inverse = jnp.sum(jnp.where(hits, slots[:, None], 0), axis=0)
    count = jnp.sum(jnp.where(owner_row == owner_index, counts_row, 0))
    ordered = jnp.take(rows_part.reshape(rows_mp, owners, order), inverse, axis=1).reshape(
        rows_mp, owners * order
    )
    left_slab = left_roots[0]
    right_slab = right_roots[0]
    zeros = jnp.zeros((rows_rep, order), jnp.float32)
    routed = lax.all_to_all(ordered, MP, split_axis=1, concat_axis=0, tiled=True)
    grad_rows = summed_on_arrival(routed.astype(jnp.float32), REPLICA, 0)
    folder = make_folder(grad_rows, left_slab, replica_index, rows_rep)
    left_term, right_term, half_dir = folder(
        (zeros, zeros, zeros), lax.all_gather(grad_rows, REPLICA, axis=0, tiled=True), jnp.int32(0)
    )
    direction = product(half_dir, lax.all_gather(right_slab, REPLICA, axis=0, tiled=True))
    new_left = decay * left_stats[0] + (1.0 - decay) * left_term
    new_right = decay * right_stats[0] + (1.0 - decay) * right_term
    grad_sq, dir_sq = (
        by_axis(jnp.sum(grad_rows * grad_rows), REPLICA_MP_REFRESH),
        by_axis(jnp.sum(direction * direction), REPLICA_MP_REFRESH),
    )
    scaled = direction * (jnp.sqrt(grad_sq) / jnp.sqrt(dir_sq + graft_eps))
    eye = jnp.eye(order, dtype=jnp.float32)
    left_full, right_full = side_by_side((new_left, new_right), REPLICA, 0, 1)
    parity = replica_index % 2
    chosen = jnp.where(parity == 0, left_full, right_full)
    scale = 2.5 / jnp.sqrt(jnp.sum(chosen * chosen))
    state = (scale**0.25 * eye, scale * chosen)

    def advance_whole(step_index, current):
        return newton_step(current[0], current[1], current[1], eye)

    iterate = run_iterations(advance_whole, state, count)[0]
    partner = replica_index + 1 - 2 * parity
    outgoing = lax.dynamic_slice_in_dim(iterate, partner * rows_rep, rows_rep, 0)
    incoming = swapped(outgoing, REPLICA, 0)
    own_rows = lax.dynamic_slice_in_dim(iterate, replica_index * rows_rep, rows_rep, 0)
    left_root = jnp.where(parity == 0, own_rows, incoming)
    right_root = jnp.where(parity == 0, incoming, own_rows)
    whole_update = gather_directly(scaled, REPLICA, 0)
    returned = lax.all_to_all(whole_update, MP, split_axis=0, concat_axis=1, tiled=True)
    update = jnp.take(returned.reshape(rows_mp, owners, order), owner_row, axis=1).reshape(
        1, rows_mp, owners * order
    )
    return (update, new_left[None], new_right[None], left_root[None], right_root[None])


def solution(mesh):
    finer = Mesh(
        mesh.devices.reshape(8, 2, 8, 2, mesh.shape["refresh"]),
        ("replica_0", "replica_1", "mp_0", "mp_1", "refresh"),
    )
    in_specs = (
        P(REPLICA, "refresh", MP, None),
        P("refresh", REPLICA, MP),
        P("refresh", REPLICA, MP),
        P("refresh", REPLICA, MP),
        P("refresh", REPLICA, MP),
        P(),
        P(),
    )
    out_specs = (
        P("refresh", MP, None),
        P("refresh", REPLICA, MP),
        P("refresh", REPLICA, MP),
        P("refresh", REPLICA, MP),
        P("refresh", REPLICA, MP),
    )
    return jax.shard_map(local, mesh=finer, in_specs=in_specs, out_specs=out_specs, check_vma=False)
```

profile of v0, /device:TPU:33, one launch (start us, length us, event | category | flops | bytes accessed | tf_op | source)
XLA Modules:
  0.0 315.0 jit_solution(1481063598009808224)
XLA Ops:
  7.2 1.4 fusion.54
  8.7 1.2 copy.25
  10.9 23.3 %all_to_all.33 = bf16[32,16,512]{2,0,1:T(8,128)(2,1)S(1)} all-to-all(bf16[32,16,512]{2,0,1:T(8,128)(2,1)S(1)} %select_bitcast_fusion), channel_id=1, replica_groups=mesh['replica_0'=8,'replica_1'=2,'mp_0'=8,'mp_1'=2,'refresh'=2] {'mp_0',..., dimensions={1} | all-to-all | bytes 1048576 | tf_op jit(solution)/shard_map/all_to_all | solution.py:111
  34.4 40.0 %all_to_all.34 = f32[16,32,512]{2,1,0:T(8,128)S(1)} all-to-all(f32[16,32,512]{2,1,0:T(8,128)S(1)} %convert_bitcast_fusion), channel_id=1, replica_groups=mesh['replica_0'=8,'replica_1'=2,'mp_0'=8,'mp_1'=2,'refresh'=2] {'replic..., dimensions={0} | all-to-all | bytes 2097152 | tf_op jit(solution)/shard_map/all_to_all | solution.py:25
  74.4 0.7 reduce_sum.58
  75.2 0.7 all-gather.9.cloned.1.call-update
  76.0 35.5 %all-gather.5.cloned.1.call-done = f32[512,512]{1,0:T(8,128)} async-done(((f32[32,512]{1,0:T(8,128)}), f32[512,512]{1,0:T(8,128)}) %all-gather.5.cloned.1.call-update) | async-done | bytes 1048592 | tf_op jit(solution)/shard_map/all_gather | solution.py:115
  111.5 2.1 fusion.43
  113.6 2.3 fusion.42
  116.0 0.7 pad_maximum_fusion
  117.3 0.7 fusion.48
  118.0 35.6 %all-gather.9.cloned.1.call-done = f32[1,512,512]{2,1,0:T(8,128)} async-done(((f32[1,32,512]{2,1,0:T(8,128)}), f32[1,512,512]{2,1,0:T(8,128)}) %all-gather.9.cloned.1.call-update) | async-done | bytes 1048592 | tf_op jit(solution)/shard_map/all_gather | solution.py:117
  153.6 2.5 multiply_reduce_fusion.1
  156.1 12.4 %all-reduce.1 = (f32[]{:T(128)}, f32[]{:T(128)}) all-reduce(f32[]{:T(128)} %multiply_reduce_fusion.2, f32[]{:T(128)} %get-tuple-element.67), channel_id=1, replica_groups=mesh['replica_0'=8,'replica_1'=2,'mp_0'=8,'mp_1'=2,'refresh'=2] {'replic..., use_global_device_ids=true, to_apply=%region_3.4 | all-reduce | flops 2 | bytes 16 | tf_op jit(solution)/shard_map/psum | solution.py:30
  168.6 6.8 %all-reduce.4 = (f32[]{:T(128)}, f32[]{:T(128)}) all-reduce(f32[]{:T(128)} %get-tuple-element.55, f32[]{:T(128)} %get-tuple-element.56), channel_id=1, replica_groups=mesh['replica_0'=8,'replica_1'=2,'mp_0'=8,'mp_1'=2,'refresh'=2] {'replic..., use_global_device_ids=true, to_apply=%region_4.5 | all-reduce | flops 2 | bytes 16 | tf_op jit(solution)/shard_map/psum | solution.py:30
  175.3 12.3 %all-reduce = (f32[]{:T(128)}, f32[]{:T(128)}) all-reduce(f32[]{:T(128)} %get-tuple-element.61, f32[]{:T(128)} %get-tuple-element.62), channel_id=1, replica_groups=mesh['replica_0'=8,'replica_1'=2,'mp_0'=8,'mp_1'=2,'refresh'=2] {'mp_0'}, use_global_device_ids=true, to_apply=%region_5.6 | all-reduce | flops 2 | bytes 16 | tf_op jit(solution)/shard_map/psum | solution.py:30
  187.6 6.0 %all-reduce.3 = (f32[]{:T(128)}, f32[]{:T(128)}) all-reduce(f32[]{:T(128)} %get-tuple-element.53, f32[]{:T(128)} %get-tuple-element.54), channel_id=1, replica_groups=mesh['replica_0'=8,'replica_1'=2,'mp_0'=8,'mp_1'=2,'refresh'=2] {'mp_1'}, use_global_device_ids=true, to_apply=%region_6.7 | all-reduce | flops 2 | bytes 16 | tf_op jit(solution)/shard_map/psum | solution.py:30
  193.6 4.4 %all-reduce.2 = (f32[]{:T(128)}, f32[]{:T(128)}) all-reduce(f32[]{:T(128)} %get-tuple-element.59, f32[]{:T(128)} %get-tuple-element.60), channel_id=1, replica_groups=mesh['replica_0'=8,'replica_1'=2,'mp_0'=8,'mp_1'=2,'refresh'=2] {'refresh'}, use_global_device_ids=true, to_apply=%region_7.8 | all-reduce | flops 2 | bytes 16 | tf_op jit(solution)/shard_map/psum | solution.py:30
  199.4 1.1 broadcast_in_dim.66
  200.5 10.9 %all-to-all-start.2 = ((f32[16,32,512]{2,1,0:T(8,128)}), f32[16,32,512]{2,1,0:T(8,128)}, u32[]{:S(2)}, u32[]{:S(2)}) async-start(f32[16,32,512]{2,1,0:T(8,128)} %broadcast_in_dim.66), calls=%async_computation.2 | async-start | bytes 2097152 | tf_op jit(solution)/shard_map/all_to_all | solution.py:46
  211.5 28.0 %all-to-all-done.2 = f32[16,32,512]{2,1,0:T(8,128)} async-done(((f32[16,32,512]{2,1,0:T(8,128)}), f32[16,32,512]{2,1,0:T(8,128)}, u32[]{:S(2)}, u32[]{:S(2)}) %all-to-all-start.2) | async-done | bytes 1048608 | tf_op jit(solution)/shard_map/all_to_all | solution.py:46
  239.5 9.1 %all-to-all-start.3 = ((f32[16,32,512]{2,1,0:T(8,128)}), f32[16,32,512]{2,1,0:T(8,128)S(1)}, u32[]{:S(2)}, u32[]{:S(2)}) async-start(f32[16,32,512]{2,1,0:T(8,128)} %all-to-all-done.2), calls=%async_computation.3 | async-start | bytes 2097152 | tf_op jit(solution)/shard_map/all_to_all | solution.py:143
  248.6 2.4 multiply_reduce_fusion
  251.9 1.8 broadcast_multiply_fusion
  253.7 48.5 %while.13 = (s32[]{:T(128)}, f32[512,512]{0,1:T(8,128)S(1)}, f32[512,512]{1,0:T(8,128)S(1)}, s32[]{:T(128)}, s32[]{:T(128)}) while((s32[]{:T(128)}, f32[512,512]{0,1:T(8,128)S(1)}, f32[512,512]{1,0:T(8,128)S(1)}, s32[]{:T(128)}, s32[]{:T(128)}) %tuple.29), condition=%wide.region_17.18_spmd.clone, body=%wide.region_16.17_spmd.clone.sunk | while | flops 8058306560 | bytes 18874428 | solution.py:74
  254.6 3.5 %fusion.91 = f32[512,512]{1,0:T(8,128)S(1)} fusion(f32[512,512]{1,0:T(8,128)S(1)} %copy.39), kind=kOutput, calls=%fused_computation.10.clone.1 | convolution fusion | flops 1611661312 | bytes 2097152 | tf_op jit(solution)/shard_map/while/body/dot_general | solution.py:63
  258.1 1.9 fusion.92
  260.0 1.9 fusion.93
  261.9 1.9 convolution_bitcast_fusion.2
  263.8 1.9 fusion.94
  266.6 3.5 %fusion.91 = f32[512,512]{1,0:T(8,128)S(1)} fusion(f32[512,512]{1,0:T(8,128)S(1)} %copy.39), kind=kOutput, calls=%fused_computation.10.clone.1 | convolution fusion | flops 1611661312 | bytes 2097152 | tf_op jit(solution)/shard_map/while/body/dot_general | solution.py:63
  270.0 1.9 fusion.92
  272.0 1.9 fusion.93
  273.9 1.9 convolution_bitcast_fusion.2
  275.8 1.9 fusion.94
  278.5 3.5 %fusion.91 = f32[512,512]{1,0:T(8,128)S(1)} fusion(f32[512,512]{1,0:T(8,128)S(1)} %copy.39), kind=kOutput, calls=%fused_computation.10.clone.1 | convolution fusion | flops 1611661312 | bytes 2097152 | tf_op jit(solution)/shard_map/while/body/dot_general | solution.py:63
  282.0 1.9 fusion.92
  283.9 1.9 fusion.93
  285.8 1.9 convolution_bitcast_fusion.2
  287.7 1.9 fusion.94
  290.4 3.5 %fusion.91 = f32[512,512]{1,0:T(8,128)S(1)} fusion(f32[512,512]{1,0:T(8,128)S(1)} %copy.39), kind=kOutput, calls=%fused_computation.10.clone.1 | convolution fusion | flops 1611661312 | bytes 2097152 | tf_op jit(solution)/shard_map/while/body/dot_general | solution.py:63
  293.9 1.9 fusion.92
  295.8 1.9 fusion.93
  297.7 1.9 convolution_bitcast_fusion.2
  299.6 1.9 fusion.94
  302.6 1.9 collective-permute-start
  306.0 1.1 broadcast_select_fusion
  307.0 1.5 select_bitcast_fusion.1
  (54 shorter events, 4.6 us)
Async XLA Ops:
  7.2 110.1 %copy-start = (f32[1,32,512]{2,1,0:T(8,128)S(1)}, f32[1,32,512]{2,1,0:T(8,128)}, u32[]{:S(2)}) copy-start(f32[1,32,512]{2,1,0:T(8,128)} %param.12) | copy-start | bytes 196612
  7.2 104.3 %all-gather.5.cloned.1.call-start = ((), (), s32[]{:S(2)}) async-start(), calls=%async_computation.4 | async-start | bytes 1114112 | tf_op jit(solution)/shard_map/all_gather | solution.py:115
  34.3 77.2 %copy-start.6 = (f32[1,32,512]{2,1,0:T(8,128)S(1)}, f32[1,32,512]{2,1,0:T(8,128)}, u32[]{:S(2)}) copy-start(f32[1,32,512]{2,1,0:T(8,128)} %param.11) | copy-start | bytes 196612
  34.4 79.2 %copy-start.7 = (f32[1,32,512]{2,1,0:T(8,128)S(1)}, f32[1,32,512]{2,1,0:T(8,128)}, u32[]{:S(2)}) copy-start(f32[1,32,512]{2,1,0:T(8,128)} %param.10) | copy-start | bytes 196612
  75.1 41.5 %copy-start.3 = (f32[32,512]{1,0:T(8,128)S(1)}, f32[32,512]{1,0:T(8,128)}, u32[]{:S(2)}) copy-start(f32[32,512]{1,0:T(8,128)} %reduce_sum.58) | copy-start | bytes 196612
  75.2 78.4 %all-gather.9.cloned.1.call-start = ((), (), s32[]{:S(2)}) async-start(), calls=%async_computation.6 | async-start | bytes 1114112 | tf_op jit(solution)/shard_map/all_gather | solution.py:117
  75.9 172.7 %all-gather.7.cloned.1.call-start = ((), (), s32[]{:S(2)}) async-start(), calls=%async_computation.5 | async-start | bytes 2228224 | tf_op jit(solution)/shard_map/all_gather | solution.py:36
  111.5 5.8 %copy-start.1 = (f32[512,512]{1,0:T(8,128)S(1)}, f32[512,512]{1,0:T(8,128)}, u32[]{:S(2)}) copy-start(f32[512,512]{1,0:T(8,128)} %all-gather.5.cloned.1.call-done) | copy-start | bytes 3145732
  113.6 85.8 %copy-start.4 = (f32[32,512]{1,0:T(8,128)}, f32[32,512]{1,0:T(8,128)S(1)}, u32[]{:S(2)}) copy-start(f32[32,512]{1,0:T(8,128)S(1)} %fusion.43) | copy-start | bytes 196612
  115.9 84.5 %copy-start.5 = (f32[32,512]{1,0:T(8,128)}, f32[32,512]{1,0:T(8,128)S(1)}, u32[]{:S(2)}) copy-start(f32[32,512]{1,0:T(8,128)S(1)} %fusion.42) | copy-start | bytes 196612
  118.0 93.5 %copy-start.8 = (s32[2,16]{1,0:T(2,128)S(1)}, s32[2,16]{1,0:T(2,128)}, u32[]{:S(2)}) copy-start(s32[2,16]{1,0:T(2,128)} %param.15) | copy-start | bytes 388
  200.5 39.0 %all-to-all-start.2 = ((f32[16,32,512]{2,1,0:T(8,128)}), f32[16,32,512]{2,1,0:T(8,128)}, u32[]{:S(2)}, u32[]{:S(2)}) async-start(f32[16,32,512]{2,1,0:T(8,128)} %broadcast_in_dim.66), calls=%async_computation.2 | async-start | bytes 2097152 | tf_op jit(solution)/shard_map/all_to_all | solution.py:46
  239.5 65.0 %all-to-all-start.3 = ((f32[16,32,512]{2,1,0:T(8,128)}), f32[16,32,512]{2,1,0:T(8,128)S(1)}, u32[]{:S(2)}, u32[]{:S(2)}) async-start(f32[16,32,512]{2,1,0:T(8,128)} %all-to-all-done.2), calls=%async_computation.3 | async-start | bytes 2097152 | tf_op jit(solution)/shard_map/all_to_all | solution.py:143
  302.5 2.6 copy-start.2
  302.6 4.5 %collective-permute-start = (f32[32,512]{1,0:T(8,128)S(1)}, f32[32,512]{1,0:T(8,128)S(1)}, u32[]{:S(2)}, u32[]{:S(2)}) collective-permute-start(f32[32,512]{1,0:T(8,128)S(1)} %constant_dynamic-slice_fusion), channel_id=1, source_target_pairs={{0,32},{32,0},{64,96},{96,64},{128,160},{160,128},{192,224},{224,1... | collective-permute-start | bytes 196616 | tf_op jit(solution)/shard_map/ppermute | solution.py:41
Sparse Core Ops, SparseCore 0:
  75.3 36.1 all-gather.4
  113.6 39.9 all-gather.8
  155.7 40.9 all-gather.6
where the time goes:
time: 317 us; the launch traced here: 315 us
  blocking collectives  105 us (33%)
  waiting for transfers between devices  99.8 us (31%)
  matrix products  52.1 us (16%)
  starting transfers between devices  22 us (7%)
  between operations  16.2 us (5%)
  other arithmetic  10.6 us (3%)
  local copies, waits for them, and re-layouts  5.64 us (2%)
  loops' own time  3.56 us (1%)
    dot_general x24, matrix products, product(): jnp.dot(left, right, precision=lax.Precision.HIGHEST, preferred_element_t...  52.1 us
    psum x5, blocking collectives, by_axis(): return functools.reduce(lax.psum, axes, shard)  41.8 us
    all_to_all x1, blocking collectives, summed_on_arrival(): lax.all_to_all(tiles, axis, split_axis=0, concat_axis=0, tiled=True)  40 us
    all_gather x1, waiting for transfers between devices, local(): lax.all_gather(right_slab, REPLICA, axis=0, tiled=True)  35.6 us
    all_gather x1, waiting for transfers between devices, local(): lax.all_gather(grad_rows, REPLICA, axis=0, tiled=True)  35.5 us
    all_to_all x1, waiting for transfers between devices, sent_to_all(): lax.all_to_all(jnp.broadcast_to(shard[None], (count, *shard.shape)), axis...  28 us
    all_to_all x1, blocking collectives, local(): lax.all_to_all(ordered, MP, split_axis=1, concat_axis=0, tiled=True)  23.3 us
    all_to_all x1, starting transfers between devices, sent_to_all(): lax.all_to_all(jnp.broadcast_to(shard[None], (count, *shard.shape)), axis...  10.9 us
  transfers between devices with their start and end apart: 6, of which 3 were waited for; matrix products, arithmetic and copies ran while one was open for 20% of the time, Pallas kernels for 0%

commit v1 on v0

v1 whole, which is shorter than its diff:
```python
import functools

import jax
import jax.numpy as jnp
from jax import lax
from jax.experimental import pallas as pl
from jax.experimental.pallas import tpu as pltpu
from jax.sharding import Mesh
from jax.sharding import PartitionSpec as P

MP = ("mp_0", "mp_1")
REPLICA = ("replica_0", "replica_1")

decay = 0.9
graft_eps = 1e-06

LANES = 128
HEAD = 8


def slot_owner(slot, part, n_long):
    return ((2 * n_long - part // 2 - slot // 2) % n_long) * 2 + slot % 2


def pair(a):
    high = a.astype(jnp.bfloat16)
    return high, (a - high.astype(jnp.float32)).astype(jnp.bfloat16)


def product(left, right, dims=((1,), (0,))):
    (lh, ll), (rh, rl) = left, right
    dot = functools.partial(
        lax.dot_general, dimension_numbers=(dims, ((), ())), preferred_element_type=jnp.float32
    )
    return dot(lh, rh) + (dot(lh, rl) + dot(ll, rh))


def mesh_place():
    owner_index = lax.axis_index("mp_0") * 2 + lax.axis_index("mp_1")
    replica_index = lax.axis_index("replica_0") * 2 + lax.axis_index("replica_1")
    return lax.axis_index("refresh"), owner_index, replica_index


def slot_columns(owner_ref, inverse_ref, group, part, slots):
    for block in range(slots):
        inverse_ref[owner_ref[group, block]] = block
    return [inverse_ref[slot_owner(slot, part, slots // 2)] for slot in range(slots)]


def bound_exponent(peak):
    return jnp.floor(jnp.log2(jnp.maximum(peak, 1e-30))) + 2.0


def coded(value, exponent):
    return jnp.round(value * jnp.exp2(23.0 - exponent)).astype(jnp.int32)


def encode(x, out_ref):
    rows = x.shape[0]
    exponent = bound_exponent(jnp.max(jnp.abs(x), axis=0, keepdims=True))
    q = coded(x, exponent)
    parts = [q[:, k * LANES : (k + 1) * LANES] for k in range(4)]
    for k in range(3):
        tail = (parts[3] >> (16 - 8 * k)) & 255
        out_ref[0:rows, k * LANES : (k + 1) * LANES] = (parts[k] << 8) | tail
    whole = exponent.astype(jnp.int32)
    out_ref[rows : rows + HEAD, :] = jnp.zeros((HEAD, 3 * LANES), jnp.int32)
    out_ref[rows : rows + 1, :] = whole[:, : 3 * LANES]
    out_ref[rows + 1 : rows + 2, :LANES] = whole[:, 3 * LANES :]


def decode(words, head, factor):
    parts = [words[:, k * LANES : (k + 1) * LANES] for k in range(3)]
    tail = (((parts[0] & 255) << 24) | ((parts[1] & 255) << 16) | ((parts[2] & 255) << 8)) >> 8
    exponents = [head[0:1, k * LANES : (k + 1) * LANES] for k in range(3)] + [head[1:2, :LANES]]
    whole = [p >> 8 for p in parts] + [tail]
    return [
        q.astype(jnp.float32) * (jnp.exp2(e.astype(jnp.float32) - 23.0) * factor)
        for q, e in zip(whole, exponents)
    ]


def order_kernel(owner_ref, rows_ref, out_ref, inverse_ref):
    group, part, _ = mesh_place()
    slots, _, order = out_ref.shape
    for slot, block in enumerate(slot_columns(owner_ref, inverse_ref, group, part, slots)):
        out_ref[slot] = rows_ref[:, pl.ds(pl.multiple_of(block * order, order), order)]


def sum_kernel(pieces_ref, out_ref):
    total = pieces_ref[0].astype(jnp.float32)
    for k in range(1, pieces_ref.shape[0]):
        total = total + pieces_ref[k].astype(jnp.float32)
    encode(total, out_ref)


def scalar_row(value):
    exponent = bound_exponent(value)
    return (
        jnp.broadcast_to(coded(value, exponent), (1, LANES)),
        jnp.broadcast_to(exponent.astype(jnp.int32), (1, LANES)),
    )


def total_sum(x):
    return jnp.sum(jnp.sum(x, axis=0, keepdims=True), axis=1, keepdims=True)


def direction_kernel(words_ref, roots_ref, grad_ref, coded_ref, norms_ref, hold_ref):
    order = grad_ref.shape[0]
    replica_index = mesh_place()[2]
    slots = words_ref.shape[0]
    rows = order // slots
    for k in range(slots):
        head = words_ref[k, rows : rows + HEAD, :]
        for c, part in enumerate(decode(words_ref[k, :rows, :], head, 1.0)):
            grad_ref[k * rows : (k + 1) * rows, c * LANES : (c + 1) * LANES] = part
    grad = grad_ref[...]
    half = product(pair(roots_ref[:, :order]), pair(grad))
    direction = product(pair(half), pair(roots_ref[:, order:]))
    hold_ref[...] = direction
    own = hold_ref[pl.ds(pl.multiple_of(replica_index * rows, rows), rows), :]
    encode(own, coded_ref)
    norms_ref[...] = jnp.zeros(norms_ref.shape, jnp.int32)
    for k, value in enumerate((total_sum(grad * grad), total_sum(direction * direction))):
        mantissa, exponent = scalar_row(value)
        for at in (coded_ref, norms_ref):
            row = rows + 2 + 2 * k if at is coded_ref else 4 + 2 * k - 2
            lane = 0 if at is coded_ref else LANES
            at[row : row + 1, lane : lane + LANES] = mantissa
            at[row + 1 : row + 2, lane : lane + LANES] = exponent


def newton_kernel(
    place_ref, owner_ref, counts_ref, grad_ref, stats_ref, mine_ref, theirs_ref,
    held_ref, factor_ref, high_ref, low_ref, rows_ref,
):
    group, owner_index, replica_index = mesh_place()
    order = grad_ref.shape[0]
    slots = counts_ref.shape[1]
    rows = order // slots
    count = jnp.int32(0)
    for block in range(slots):
        count = count + jnp.where(owner_ref[group, block] == owner_index, counts_ref[group, block], 0)
    parity = replica_index % 2
    grad = pair(grad_ref[...])

    def new_stats(term):
        held_ref[...] = decay * stats_ref[...] + (1.0 - decay) * term

    @pl.when(parity == 0)
    def _():
        new_stats(product(grad, grad, ((1,), (1,))))

    @pl.when(parity == 1)
    def _():
        new_stats(product(grad, grad, ((0,), (0,))))

    own = pl.multiple_of(replica_index * rows, rows)
    other = pl.multiple_of((replica_index + 1 - 2 * parity) * rows, rows)
    both = pl.multiple_of((replica_index - parity) * rows, 2 * rows)
    mine_ref[:rows, :] = held_ref[pl.ds(own, rows), :]
    theirs_ref[:rows, :] = held_ref[pl.ds(other, rows), :]
    full = held_ref[...]
    scale = 2.5 / jnp.sqrt(total_sum(full * full))
    held_ref[...] = scale * full
    start = jnp.sqrt(jnp.sqrt(scale))
    eye5 = jnp.where(
        lax.broadcasted_iota(jnp.int32, (order, order), 0)
        == lax.broadcasted_iota(jnp.int32, (order, order), 1),
        5.0,
        0.0,
    )

    def advance(step, carry):
        factor = (eye5 - held_ref[...]) * 0.25
        factor_ref[...] = factor
        split = pair(factor)

        @pl.when(step == 0)
        def _():
            rows_ref[...] = start * factor_ref[pl.ds(both, 2 * rows), :]

        @pl.when(step > 0)
        def _():
            rows_ref[...] = product(pair(rows_ref[...]), split)

        @pl.when(step < count - 1)
        def _():
            square = product(split, split)
            high_ref[...], low_ref[...] = pair(square)
            second = (high_ref[...], low_ref[...])
            fourth = product(second, second)
            high_ref[...], low_ref[...] = pair(fourth)
            held_ref[...] = product(pair(held_ref[...]), (high_ref[...], low_ref[...]))

        return carry

    lax.fori_loop(0, count, advance, jnp.int32(0))
    mine_ref[rows:, :] = rows_ref[pl.ds(pl.multiple_of(parity * rows, rows), rows), :]
    theirs_ref[rows:, :] = rows_ref[pl.ds(pl.multiple_of((1 - parity) * rows, rows), rows), :]


def finish_kernel(
    owner_ref, words_ref, mine_ref, theirs_ref,
    update_ref, left_ref, right_ref, left_root_ref, right_root_ref, inverse_ref,
):
    group, part, replica_index = mesh_place()
    slots = words_ref.shape[0]
    rows = words_ref.shape[1] - HEAD
    order = 4 * LANES

    def total(row):
        result = jnp.zeros((1, LANES), jnp.float32)
        for k in range(slots):
            for lane in (0, LANES):
                mantissa = words_ref[k, rows + row : rows + row + 1, lane : lane + LANES]
                exponent = words_ref[k, rows + row + 1 : rows + row + 2, lane : lane + LANES]
                result = result + mantissa.astype(jnp.float32) * jnp.exp2(
                    exponent.astype(jnp.float32) - 23.0
                )
        return result

    factor = jnp.sqrt(total(2)) / jnp.sqrt(total(4) + graft_eps)
    for slot, block in enumerate(slot_columns(owner_ref, inverse_ref, group, part, slots)):
        head = words_ref[slot, rows : rows + HEAD, :]
        base = pl.multiple_of(block * order, order)
        for c, piece in enumerate(decode(words_ref[slot, :rows, :], head, factor)):
            update_ref[:, pl.ds(pl.multiple_of(base + c * LANES, LANES), LANES)] = piece
    even = replica_index % 2 == 0
    mine, theirs = mine_ref[...], theirs_ref[...]
    left = jnp.where(even, mine, theirs)
    right = jnp.where(even, theirs, mine)
    left_ref[...], left_root_ref[...] = left[:rows], left[rows:]
    right_ref[...], right_root_ref[...] = right[:rows], right[rows:]


VMEM = pl.BlockSpec(memory_space=pltpu.VMEM)
SMEM = pl.BlockSpec(memory_space=pltpu.SMEM)


def local(grad_partial, left_stats, right_stats, left_roots, right_roots, newton_counts, owner):
    owners = lax.axis_size(MP)
    replicas = lax.axis_size(REPLICA)
    rows_part = grad_partial[0, 0]
    rows = rows_part.shape[0]
    order = rows_part.shape[1] // owners
    f32, i32 = jnp.float32, jnp.int32
    shape = jax.ShapeDtypeStruct

    inputs = jnp.concatenate([left_roots[0], right_roots[0], left_stats[0], right_stats[0]], axis=1)
    gathered = lax.all_gather(inputs, REPLICA, axis=0, tiled=True)

    ordered = pl.pallas_call(
        order_kernel,
        out_shape=shape((owners, rows, order), jnp.bfloat16),
        in_specs=[SMEM, VMEM],
        out_specs=VMEM,
        scratch_shapes=[pltpu.SMEM((owners,), i32)],
        name="order_blocks",
    )(owner, rows_part)
    arrived = lax.all_to_all(ordered, REPLICA, 0, 0, tiled=True)
    summed = pl.pallas_call(
        sum_kernel,
        out_shape=shape((rows + HEAD, 3 * LANES), i32),
        in_specs=[VMEM],
        out_specs=VMEM,
        name="sum_partials",
    )(arrived)

    there = [
        (slot * owners + part, part * owners + slot_owner(slot, part, owners // 2))
        for slot in range(replicas)
        for part in range(owners)
    ]
    back = [(b, a) for a, b in there]
    summed = lax.ppermute(summed, REPLICA + MP, there)
    words = lax.all_gather(summed, REPLICA, axis=0, tiled=False)

    grad, coded_rows, norms = pl.pallas_call(
        direction_kernel,
        grid=(1,),
        out_shape=(
            shape((order, order), f32),
            shape((rows + HEAD, 3 * LANES), i32),
            shape((HEAD, 3 * LANES), i32),
        ),
        in_specs=[VMEM, pl.BlockSpec((order, 2 * order), lambda i: (0, 0))],
        out_specs=(VMEM, VMEM, VMEM),
        scratch_shapes=[pltpu.VMEM((order, order), f32)],
        cost_estimate=pl.CostEstimate(
            flops=12 * order**3, bytes_accessed=20 * order**2, transcendentals=0
        ),
        name="direction",
    )(words, gathered)

    coded_rows = lax.ppermute(coded_rows, REPLICA + MP, back)
    crossed = [(2 * a + f, 2 * b + 1 - f) for a, b in back for f in (0, 1)]
    norms = lax.ppermute(norms, REPLICA + MP + ("refresh",), crossed)
    place = lax.axis_index(REPLICA) % 2

    mine, theirs = pl.pallas_call(
        newton_kernel,
        grid_spec=pltpu.PrefetchScalarGridSpec(
            num_scalar_prefetch=1,
            grid=(1,),
            in_specs=[
                SMEM,
                SMEM,
                VMEM,
                pl.BlockSpec((order, order), lambda i, parity: (0, 2 + parity[0])),
            ],
            out_specs=[VMEM, VMEM],
            scratch_shapes=[
                pltpu.VMEM((order, order), f32),
                pltpu.VMEM((order, order), f32),
                pltpu.VMEM((order, order), jnp.bfloat16),
                pltpu.VMEM((order, order), jnp.bfloat16),
                pltpu.VMEM((2 * rows, order), f32),
            ],
        ),
        out_shape=(shape((2 * rows, order), f32), shape((2 * rows, order), f32)),
        cost_estimate=pl.CostEstimate(
            flops=90 * order**3, bytes_accessed=8 * order**2, transcendentals=0
        ),
        name="newton",
    )(place.reshape(1), owner, newton_counts, grad, gathered)
    theirs = lax.ppermute(theirs, REPLICA, [(i, i ^ 1) for i in range(replicas)])

    payload = jnp.concatenate([coded_rows[:rows], coded_rows[rows:] + norms], axis=0)
    words = lax.all_gather(payload, REPLICA, axis=0, tiled=False)

    outs = pl.pallas_call(
        finish_kernel,
        out_shape=(shape((rows, owners * order), f32),) + (shape((rows, order), f32),) * 4,
        in_specs=[SMEM, VMEM, VMEM, VMEM],
        out_specs=(VMEM,) * 5,
        scratch_shapes=[pltpu.SMEM((owners,), i32)],
        name="finish",
    )(owner, words, mine, theirs)
    return tuple(out[None] for out in outs)


def solution(mesh):
    finer = Mesh(
        mesh.devices.reshape(8, 2, 8, 2, mesh.shape["refresh"]),
        ("replica_0", "replica_1", "mp_0", "mp_1", "refresh"),
    )
    in_specs = (
        P(REPLICA, "refresh", MP, None),
        P("refresh", REPLICA, MP),
        P("refresh", REPLICA, MP),
        P("refresh", REPLICA, MP),
        P("refresh", REPLICA, MP),
        P(),
        P(),
    )
    out_specs = (
        P("refresh", MP, None),
        P("refresh", REPLICA, MP),
        P("refresh", REPLICA, MP),
        P("refresh", REPLICA, MP),
        P("refresh", REPLICA, MP),
    )
    return jax.shard_map(local, mesh=finer, in_specs=in_specs, out_specs=out_specs, check_vma=False)
```

time: 317 us -> 142 us (0.45)
  the two profiles are of different devices: /device:TPU:33 before, /device:TPU:53 now
where the time goes in v1:
time: 142 us; the launch traced here: 140 us
  blocking collectives  74.6 us (53%)
  Pallas kernels  24.9 us (18%)
  starting transfers between devices  17.5 us (12%)
  between operations  14.1 us (10%)
  waiting for transfers between devices  6.57 us (5%)
  other arithmetic  1.68 us (1%)
    all_to_all x1, blocking collectives, local(): arrived = lax.all_to_all(ordered, REPLICA, 0, 0, tiled=True)  30.4 us
    all_gather x1, blocking collectives, local(): words = lax.all_gather(summed, REPLICA, axis=0, tiled=False)  23.4 us
    all_gather x1, blocking collectives, local(): words = lax.all_gather(payload, REPLICA, axis=0, tiled=False)  20.8 us
    pallas_call x1, Pallas kernels, local(): pl.pallas_call(newton_kernel, grid_spec=pltpu.PrefetchScalarGridSpec(num_...  14.1 us
    ppermute x1, starting transfers between devices, local(): coded_rows = lax.ppermute(coded_rows, REPLICA + MP, back)  7.89 us
    ppermute x1, waiting for transfers between devices, local(): summed = lax.ppermute(summed, REPLICA + MP, there)  6.55 us
    pallas_call x1, Pallas kernels, local(): pl.pallas_call(direction_kernel, grid=(1,), out_shape=(shape((order, orde...  4.55 us
    ppermute x1, starting transfers between devices, local(): lax.ppermute(theirs, REPLICA, [(i, i ^ 1) for i in range(replicas)])  3.84 us
  transfers between devices with their start and end apart: 5, of which 1 were waited for; matrix products, arithmetic and copies ran while one was open for 0% of the time, Pallas kernels for 13%

profile of v1, /device:TPU:53, one launch (start us, length us, event | category | flops | bytes accessed | tf_op | source)
XLA Modules:
  0.0 140.1 jit_solution(7586590938604008252)
XLA Ops:
  7.2 0.0 all-gather.4.cloned.1.call-start
  7.2 1.7 %pad_maximum_fusion = f32[32,2048]{1,0:T(8,128)} fusion(f32[32,512]{1,0:T(8,128)} %bitcast.16, f32[32,512]{1,0:T(8,128)} %bitcast.17, f32[32,512]{1,0:T(8,128)} %bitcast.18, f32[32,512]{1,0:T(8,128)} %bitcast.19), kind=kLoop, calls=%fused_computation | loop fusion | flops 196608 | bytes 524288 | tf_op jit(solution)/shard_map/concatenate | solution.py:251
  8.9 0.0 all-gather.4.cloned.1.call-update
  8.9 1.9 %order_blocks.1 = bf16[16,32,512]{2,1,0:T(8,128)(2,1)} custom-call(s32[2,16]{1,0:T(2,128)} %owner_ref.5, bf16[32,8192]{1,0:T(8,128)(2,1)} %bitcast.15), custom_call_target="tpu_custom_call" | custom-call | tf_op jit(solution)/shard_map/order_blocks/pallas_call | solution.py:254
  10.8 30.4 %all_to_all.5.pieces_ref = bf16[16,32,512]{2,1,0:T(8,128)(2,1)} all-to-all(bf16[16,32,512]{2,1,0:T(8,128)(2,1)} %order_blocks.1), channel_id=1, replica_groups=mesh['replica_0'=8,'replica_1'=2,'mp_0'=8,'mp_1'=2,'refresh'=2] {'replic..., dimensions={0} | all-to-all | bytes 1048576 | tf_op jit(solution)/shard_map/all_to_all | solution.py:262
  41.3 1.8 %sum_partials.1 = s32[40,384]{1,0:T(8,128)} custom-call(bf16[16,32,512]{2,1,0:T(8,128)(2,1)} %all_to_all.5.pieces_ref), custom_call_target="tpu_custom_call" | custom-call | tf_op jit(solution)/shard_map/sum_partials/pallas_call | solution.py:263
  43.0 3.8 %collective-permute-start = (s32[40,384]{1,0:T(8,128)}, s32[40,384]{1,0:T(8,128)S(1)}, u32[]{:S(2)}, u32[]{:S(2)}) collective-permute-start(s32[40,384]{1,0:T(8,128)} %sum_partials.1), channel_id=1, source_target_pairs={{0,0},{2,32},{4,92},{6,124},{8,152},{10,184},{12,212},{14,244},{16... | collective-permute-start | bytes 184328 | tf_op jit(solution)/shard_map/ppermute | solution.py:277
  46.9 6.5 %collective-permute-done = s32[40,384]{1,0:T(8,128)S(1)} collective-permute-done((s32[40,384]{1,0:T(8,128)}, s32[40,384]{1,0:T(8,128)S(1)}, u32[]{:S(2)}, u32[]{:S(2)}) %collective-permute-start) | collective-permute-done | bytes 61472 | tf_op jit(solution)/shard_map/ppermute | solution.py:277
  53.4 23.4 %all-gather = s32[640,384]{1,0:T(8,128)} all-gather(s32[40,384]{1,0:T(8,128)S(1)} %collective-permute-done), channel_id=2, replica_groups=mesh['replica_0'=8,'replica_1'=2,'mp_0'=8,'mp_1'=2,'refresh'=2] {'replic..., dimensions={0}, use_global_device_ids=true | all-gather | bytes 1044480 | tf_op jit(solution)/shard_map/all_gather | solution.py:278
  76.8 0.0 all-gather.4.cloned.1.call-done.roots_ref.stats_ref
  76.8 4.5 %direction.1 = (f32[512,512]{1,0:T(8,128)}, s32[40,384]{1,0:T(8,128)}, s32[8,384]{1,0:T(8,128)}) custom-call(s32[16,40,384]{2,1,0:T(8,128)} %bitcast.14, f32[512,2048]{1,0:T(8,128)} %all-gather.4.cloned.1.call-done.roots_ref.stats_ref), custom_call_target="tpu_custom_call" | custom-call | flops 1610612736 | bytes 5242880 | tf_op jit(solution)/shard_map/direction/pallas_call | solution.py:280
  81.4 1.9 %collective-permute-start.2 = (s32[8,384]{1,0:T(8,128)}, s32[8,384]{1,0:T(8,128)S(1)}, u32[]{:S(2)}, u32[]{:S(2)}) collective-permute-start(s32[8,384]{1,0:T(8,128)} %get-tuple-element.16), channel_id=1, source_target_pairs={{0,1},{1,0},{32,3},{33,2},{92,5},{93,4},{124,7},{125,6},{152,9},{1... | collective-permute-start | bytes 36872 | tf_op jit(solution)/shard_map/ppermute | solution.py:299
  83.3 7.9 %collective-permute-start.1 = (s32[40,384]{1,0:T(8,128)}, s32[40,384]{1,0:T(8,128)S(1)}, u32[]{:S(2)}, u32[]{:S(2)}) collective-permute-start(s32[40,384]{1,0:T(8,128)} %get-tuple-element.15), channel_id=1, source_target_pairs={{0,0},{32,2},{92,4},{124,6},{152,8},{184,10},{212,12},{244,14},{27... | collective-permute-start | bytes 184328 | tf_op jit(solution)/shard_map/ppermute | solution.py:297
  91.2 14.1 %newton.1 = (f32[64,512]{1,0:T(8,128)}, f32[64,512]{1,0:T(8,128)}) custom-call(s32[1]{0:T(128)} %bitcast.7.place_ref, s32[2,16]{1,0:T(2,128)} %owner_ref.5, s32[2,16]{1,0:T(2,128)} %counts_ref.1, f32[512,512]{1,0:T(8,128)} %get-tuple-element.17.grad_ref, f32[512,2048]{1,0:T(8,128)} %all-gather.4.cloned.1.call-done.roots_ref.stats_ref), custom_call_target="tpu_custom_call" | custom-call | flops 12079595520 | bytes 2097152 | tf_op jit(solution)/shard_map/newton/pallas_call | solution.py:302
  105.3 3.8 %collective-permute-start.3 = (f32[64,512]{1,0:T(8,128)}, f32[64,512]{1,0:T(8,128)S(1)}, u32[]{:S(2)}, u32[]{:S(2)}) collective-permute-start(f32[64,512]{1,0:T(8,128)} %get-tuple-element.19), channel_id=1, source_target_pairs={{0,32},{32,0},{64,96},{96,64},{128,160},{160,128},{192,224},{224,1... | collective-permute-start | bytes 393224 | tf_op jit(solution)/shard_map/ppermute | solution.py:328
  109.1 0.0 collective-permute-done.1
  109.1 0.0 collective-permute-done.2
  109.2 20.8 %all-gather.1 = s32[640,384]{1,0:T(8,128)} all-gather(s32[40,384]{1,0:T(8,128)S(1)} %pad_add_fusion), channel_id=3, replica_groups=mesh['replica_0'=8,'replica_1'=2,'mp_0'=8,'mp_1'=2,'refresh'=2] {'replic..., dimensions={0}, use_global_device_ids=true | all-gather | bytes 1044480 | tf_op jit(solution)/shard_map/all_gather | solution.py:331
  130.0 0.0 collective-permute-done.3.theirs_ref
  130.0 0.0 copy-start
  130.0 0.7 copy-done
  130.6 2.6 %finish.1 = (f32[32,8192]{1,0:T(8,128)}, f32[32,512]{1,0:T(8,128)}, f32[32,512]{1,0:T(8,128)}, f32[32,512]{1,0:T(8,128)}, f32[32,512]{1,0:T(8,128)}) custom-call(s32[2,16]{1,0:T(2,128)} %owner_ref.5, s32[16,40,384]{2,1,0:T(8,128)} %bitcast.13, f32[64,512]{1,0:T(8,128)} %get-tuple-element.18.mine_ref, f32[64,512]{1,0:T(8,128)} %copy-done), custom_call_target="tpu_custom_call" | custom-call | tf_op jit(solution)/shard_map/finish/pallas_call | solution.py:333
  (3 shorter events, 0.0 us)
Async XLA Ops:
  7.2 69.7 %all-gather.4.cloned.1.call-start = ((), (), s32[]{:S(2)}) async-start(), calls=%async_computation.1 | async-start | bytes 4456448 | tf_op jit(solution)/shard_map/all_gather | solution.py:252
  43.0 10.4 %collective-permute-start = (s32[40,384]{1,0:T(8,128)}, s32[40,384]{1,0:T(8,128)S(1)}, u32[]{:S(2)}, u32[]{:S(2)}) collective-permute-start(s32[40,384]{1,0:T(8,128)} %sum_partials.1), channel_id=1, source_target_pairs={{0,0},{2,32},{4,92},{6,124},{8,152},{10,184},{12,212},{14,244},{16... | collective-permute-start | bytes 184328 | tf_op jit(solution)/shard_map/ppermute | solution.py:277
  81.4 27.7 %collective-permute-start.2 = (s32[8,384]{1,0:T(8,128)}, s32[8,384]{1,0:T(8,128)S(1)}, u32[]{:S(2)}, u32[]{:S(2)}) collective-permute-start(s32[8,384]{1,0:T(8,128)} %get-tuple-element.16), channel_id=1, source_target_pairs={{0,1},{1,0},{32,3},{33,2},{92,5},{93,4},{124,7},{125,6},{152,9},{1... | collective-permute-start | bytes 36872 | tf_op jit(solution)/shard_map/ppermute | solution.py:299
  83.3 25.8 %collective-permute-start.1 = (s32[40,384]{1,0:T(8,128)}, s32[40,384]{1,0:T(8,128)S(1)}, u32[]{:S(2)}, u32[]{:S(2)}) collective-permute-start(s32[40,384]{1,0:T(8,128)} %get-tuple-element.15), channel_id=1, source_target_pairs={{0,0},{32,2},{92,4},{124,6},{152,8},{184,10},{212,12},{244,14},{27... | collective-permute-start | bytes 184328 | tf_op jit(solution)/shard_map/ppermute | solution.py:297
  105.3 24.7 %collective-permute-start.3 = (f32[64,512]{1,0:T(8,128)}, f32[64,512]{1,0:T(8,128)S(1)}, u32[]{:S(2)}, u32[]{:S(2)}) collective-permute-start(f32[64,512]{1,0:T(8,128)} %get-tuple-element.19), channel_id=1, source_target_pairs={{0,32},{32,0},{64,96},{96,64},{128,160},{160,128},{192,224},{224,1... | collective-permute-start | bytes 393224 | tf_op jit(solution)/shard_map/ppermute | solution.py:328
  130.0 0.7 copy-start
Sparse Core Ops, SparseCore 0:
  10.1 56.0 all-gather.3

commit v2 on v1

--- a/solution.py
+++ b/solution.py
@@ -19,7 +19,7 @@
 
 
 def slot_owner(slot, part, n_long):
-    return ((2 * n_long - part // 2 - slot // 2) % n_long) * 2 + slot % 2
+    return ((2 * (part // 2) + n_long // 2 - slot // 2 + n_long) % n_long) * 2 + slot % 2
 
 
 def pair(a):
@@ -80,9 +80,26 @@
     ]
 
 
-def order_kernel(owner_ref, rows_ref, out_ref, inverse_ref):
+def encode_narrow(x, write):
+    exponent = bound_exponent(jnp.max(jnp.abs(x), axis=0, keepdims=True)) - 1.0
+    limit = 32767.0
+    q = jnp.round(x * jnp.exp2(15.0 - exponent))
+    q = jnp.clip(q, -limit, limit).astype(jnp.int32)
+    half = x.shape[1] // 2
+    write(0, (q[:, :half] << 16) | (q[:, half:] & 65535))
+    whole = exponent.astype(jnp.int32)
+    write(x.shape[0], whole[:, :half])
+    write(x.shape[0] + 1, whole[:, half:])
+
+
+def order_kernel(
+    owner_ref, rows_ref, left_stats_ref, right_stats_ref, left_roots_ref, right_roots_ref,
+    out_ref, inputs_ref, inverse_ref,
+):
     group, part, _ = mesh_place()
     slots, _, order = out_ref.shape
+    for k, ref in enumerate((left_roots_ref, right_roots_ref, left_stats_ref, right_stats_ref)):
+        inputs_ref[:, k * order : (k + 1) * order] = ref[...]
     for slot, block in enumerate(slot_columns(owner_ref, inverse_ref, group, part, slots)):
         out_ref[slot] = rows_ref[:, pl.ds(pl.multiple_of(block * order, order), order)]
 
@@ -106,44 +123,68 @@
     return jnp.sum(jnp.sum(x, axis=0, keepdims=True), axis=1, keepdims=True)
 
 
-def direction_kernel(words_ref, roots_ref, grad_ref, coded_ref, norms_ref, hold_ref):
+def direction_kernel(
+    words_ref, inputs_ref, out_ref, coded_ref,
+    grad_ref, left_ref, right_ref, hold_ref, left_sem, right_sem, grad_sem,
+):
     order = grad_ref.shape[0]
-    replica_index = mesh_place()[2]
     slots = words_ref.shape[0]
     rows = order // slots
+    left_copy = pltpu.make_async_copy(inputs_ref.at[:, :order], left_ref, left_sem)
+    right_copy = pltpu.make_async_copy(inputs_ref.at[:, order : 2 * order], right_ref, right_sem)
+    left_copy.start()
+    right_copy.start()
     for k in range(slots):
         head = words_ref[k, rows : rows + HEAD, :]
         for c, part in enumerate(decode(words_ref[k, :rows, :], head, 1.0)):
             grad_ref[k * rows : (k + 1) * rows, c * LANES : (c + 1) * LANES] = part
+    grad_copy = pltpu.make_async_copy(grad_ref, out_ref, grad_sem)
+    grad_copy.start()
     grad = grad_ref[...]
-    half = product(pair(roots_ref[:, :order]), pair(grad))
-    direction = product(pair(half), pair(roots_ref[:, order:]))
+    left_copy.wait()
+    half = product(pair(left_ref[...]), pair(grad))
+    right_copy.wait()
+    direction = product(pair(half), pair(right_ref[...]))
     hold_ref[...] = direction
-    own = hold_ref[pl.ds(pl.multiple_of(replica_index * rows, rows), rows), :]
-    encode(own, coded_ref)
-    norms_ref[...] = jnp.zeros(norms_ref.shape, jnp.int32)
-    for k, value in enumerate((total_sum(grad * grad), total_sum(direction * direction))):
-        mantissa, exponent = scalar_row(value)
-        for at in (coded_ref, norms_ref):
-            row = rows + 2 + 2 * k if at is coded_ref else 4 + 2 * k - 2
-            lane = 0 if at is coded_ref else LANES
-            at[row : row + 1, lane : lane + LANES] = mantissa
-            at[row + 1 : row + 2, lane : lane + LANES] = exponent
+    norms = [scalar_row(total_sum(x * x)) for x in (grad, direction)]
+    for k in range(slots):
+
+        def write(at, value):
+            coded_ref[k, at : at + value.shape[0], :] = value
+
+        encode_narrow(hold_ref[k * rows : (k + 1) * rows, :], write)
+        for n, parts in enumerate(norms):
+            write(rows + 2 + n, jnp.concatenate(parts, axis=1))
+        write(rows + 4, jnp.zeros((HEAD - 4, 2 * LANES), jnp.int32))
+    grad_copy.wait()
+
+
+def totals_of(returned, rows):
+    lines = returned[:, rows + 2 : rows + 4, :]
+    exponent = lines[:, :, LANES:].astype(jnp.float32) - 23.0
+    return jnp.sum(lines[:, :, :LANES].astype(jnp.float32) * jnp.exp2(exponent), axis=0)
 
 
 def newton_kernel(
-    place_ref, owner_ref, counts_ref, grad_ref, stats_ref, mine_ref, theirs_ref,
-    held_ref, factor_ref, high_ref, low_ref, rows_ref,
+    owner_ref, counts_ref, grad_ref, inputs_ref, mine_ref, theirs_ref,
+    stats_ref, held_ref, factor_ref, high_ref, low_ref, rows_ref, grad_sem, stats_sem,
 ):
     group, owner_index, replica_index = mesh_place()
     order = grad_ref.shape[0]
+    grad_copy = pltpu.make_async_copy(grad_ref, factor_ref, grad_sem)
+    grad_copy.start()
     slots = counts_ref.shape[1]
     rows = order // slots
     count = jnp.int32(0)
     for block in range(slots):
         count = count + jnp.where(owner_ref[group, block] == owner_index, counts_ref[group, block], 0)
     parity = replica_index % 2
-    grad = pair(grad_ref[...])
+    side = pl.ds(pl.multiple_of((2 + parity) * order, order), order)
+    stats_copy = pltpu.make_async_copy(inputs_ref.at[:, side], stats_ref, stats_sem)
+    stats_copy.start()
+    grad_copy.wait()
+    grad = pair(factor_ref[...])
+    stats_copy.wait()
 
     def new_stats(term):
         held_ref[...] = decay * stats_ref[...] + (1.0 - decay) * term
@@ -202,31 +243,26 @@
 
 
 def finish_kernel(
-    owner_ref, words_ref, mine_ref, theirs_ref,
-    update_ref, left_ref, right_ref, left_root_ref, right_root_ref, inverse_ref,
+    owner_ref, words_ref, totals_ref, others_ref, mine_ref, theirs_ref,
+    update_ref, left_ref, right_ref, left_root_ref, right_root_ref,
 ):
-    group, part, replica_index = mesh_place()
+    group, _, replica_index = mesh_place()
     slots = words_ref.shape[0]
     rows = words_ref.shape[1] - HEAD
     order = 4 * LANES
-
-    def total(row):
-        result = jnp.zeros((1, LANES), jnp.float32)
-        for k in range(slots):
-            for lane in (0, LANES):
-                mantissa = words_ref[k, rows + row : rows + row + 1, lane : lane + LANES]
-                exponent = words_ref[k, rows + row + 1 : rows + row + 2, lane : lane + LANES]
-                result = result + mantissa.astype(jnp.float32) * jnp.exp2(
-                    exponent.astype(jnp.float32) - 23.0
+    totals = totals_ref[...] + others_ref[...]
+    factor = jnp.sqrt(totals[0:1, :]) / jnp.sqrt(totals[1:2, :] + graft_eps)
+    for block in range(slots):
+        slot = owner_ref[group, block]
+        for c in range(2):
+            lanes = slice(c * LANES, (c + 1) * LANES)
+            words = words_ref[slot, :rows, lanes]
+            for h, q in enumerate((words >> 16, (words << 16) >> 16)):
+                exponent = words_ref[slot, rows + h : rows + h + 1, lanes].astype(jnp.float32)
+                base = block * order + (2 * h + c) * LANES
+                update_ref[:, base : base + LANES] = q.astype(jnp.float32) * (
+                    jnp.exp2(exponent - 15.0) * factor
                 )
-        return result
-
-    factor = jnp.sqrt(total(2)) / jnp.sqrt(total(4) + graft_eps)
-    for slot, block in enumerate(slot_columns(owner_ref, inverse_ref, group, part, slots)):
-        head = words_ref[slot, rows : rows + HEAD, :]
-        base = pl.multiple_of(block * order, order)
-        for c, piece in enumerate(decode(words_ref[slot, :rows, :], head, factor)):
-            update_ref[:, pl.ds(pl.multiple_of(base + c * LANES, LANES), LANES)] = piece
     even = replica_index % 2 == 0
     mine, theirs = mine_ref[...], theirs_ref[...]
     left = jnp.where(even, mine, theirs)
@@ -237,6 +273,11 @@
 
 VMEM = pl.BlockSpec(memory_space=pltpu.VMEM)
 SMEM = pl.BlockSpec(memory_space=pltpu.SMEM)
+ANY = pl.BlockSpec(memory_space=pl.ANY)
+
+
+def on_chip(array):
+    return pltpu.with_memory_space_constraint(array, pltpu.VMEM)
 
 
 def local(grad_partial, left_stats, right_stats, left_roots, right_roots, newton_counts, owner):
@@ -248,96 +289,80 @@
     f32, i32 = jnp.float32, jnp.int32
     shape = jax.ShapeDtypeStruct
 
-    inputs = jnp.concatenate([left_roots[0], right_roots[0], left_stats[0], right_stats[0]], axis=1)
-    gathered = lax.all_gather(inputs, REPLICA, axis=0, tiled=True)
-
-    ordered = pl.pallas_call(
+    ordered, inputs = pl.pallas_call(
         order_kernel,
-        out_shape=shape((owners, rows, order), jnp.bfloat16),
-        in_specs=[SMEM, VMEM],
-        out_specs=VMEM,
+        out_shape=(pltpu.VMEM((owners, rows, order), jnp.bfloat16), shape((rows, 4 * order), f32)),
+        in_specs=[SMEM] + [VMEM] * 5,
+        out_specs=(VMEM, VMEM),
         scratch_shapes=[pltpu.SMEM((owners,), i32)],
         name="order_blocks",
-    )(owner, rows_part)
+    )(owner, rows_part, left_stats[0], right_stats[0], left_roots[0], right_roots[0])
+    gathered = lax.all_gather(inputs, REPLICA, axis=0, tiled=True)
     arrived = lax.all_to_all(ordered, REPLICA, 0, 0, tiled=True)
     summed = pl.pallas_call(
         sum_kernel,
-        out_shape=shape((rows + HEAD, 3 * LANES), i32),
+        out_shape=pltpu.VMEM((rows + HEAD, 3 * LANES), i32),
         in_specs=[VMEM],
         out_specs=VMEM,
         name="sum_partials",
-    )(arrived)
+    )(on_chip(arrived))
 
     there = [
         (slot * owners + part, part * owners + slot_owner(slot, part, owners // 2))
         for slot in range(replicas)
         for part in range(owners)
     ]
-    back = [(b, a) for a, b in there]
     summed = lax.ppermute(summed, REPLICA + MP, there)
     words = lax.all_gather(summed, REPLICA, axis=0, tiled=False)
 
-    grad, coded_rows, norms = pl.pallas_call(
+    grad, coded_blocks = pl.pallas_call(
         direction_kernel,
-        grid=(1,),
         out_shape=(
             shape((order, order), f32),
-            shape((rows + HEAD, 3 * LANES), i32),
-            shape((HEAD, 3 * LANES), i32),
+            shape((owners, rows + HEAD, 2 * LANES), i32),
         ),
-        in_specs=[VMEM, pl.BlockSpec((order, 2 * order), lambda i: (0, 0))],
-        out_specs=(VMEM, VMEM, VMEM),
-        scratch_shapes=[pltpu.VMEM((order, order), f32)],
+        in_specs=[VMEM, ANY],
+        out_specs=(ANY, VMEM),
+        scratch_shapes=[pltpu.VMEM((order, order), f32)] * 4 + [pltpu.SemaphoreType.DMA] * 3,
         cost_estimate=pl.CostEstimate(
             flops=12 * order**3, bytes_accessed=20 * order**2, transcendentals=0
         ),
         name="direction",
-    )(words, gathered)
-
-    coded_rows = lax.ppermute(coded_rows, REPLICA + MP, back)
-    crossed = [(2 * a + f, 2 * b + 1 - f) for a, b in back for f in (0, 1)]
-    norms = lax.ppermute(norms, REPLICA + MP + ("refresh",), crossed)
-    place = lax.axis_index(REPLICA) % 2
+    )(on_chip(words), gathered)
+    returned = lax.all_to_all(coded_blocks, MP, 0, 0, tiled=True)
 
     mine, theirs = pl.pallas_call(
         newton_kernel,
-        grid_spec=pltpu.PrefetchScalarGridSpec(
-            num_scalar_prefetch=1,
-            grid=(1,),
-            in_specs=[
-                SMEM,
-                SMEM,
-                VMEM,
-                pl.BlockSpec((order, order), lambda i, parity: (0, 2 + parity[0])),
-            ],
-            out_specs=[VMEM, VMEM],
-            scratch_shapes=[
-                pltpu.VMEM((order, order), f32),
-                pltpu.VMEM((order, order), f32),
-                pltpu.VMEM((order, order), jnp.bfloat16),
-                pltpu.VMEM((order, order), jnp.bfloat16),
-                pltpu.VMEM((2 * rows, order), f32),
-            ],
-        ),
-        out_shape=(shape((2 * rows, order), f32), shape((2 * rows, order), f32)),
+        in_specs=[SMEM, SMEM, ANY, ANY],
+        out_specs=[VMEM, VMEM],
+        scratch_shapes=[
+            pltpu.VMEM((order, order), f32),
+            pltpu.VMEM((order, order), f32),
+            pltpu.VMEM((order, order), f32),
+            pltpu.VMEM((order, order), jnp.bfloat16),
+            pltpu.VMEM((order, order), jnp.bfloat16),
+            pltpu.VMEM((2 * rows, order), f32),
+            pltpu.SemaphoreType.DMA,
+            pltpu.SemaphoreType.DMA,
+        ],
+        out_shape=(pltpu.VMEM((2 * rows, order), f32), pltpu.VMEM((2 * rows, order), f32)),
         cost_estimate=pl.CostEstimate(
             flops=90 * order**3, bytes_accessed=8 * order**2, transcendentals=0
         ),
         name="newton",
-    )(place.reshape(1), owner, newton_counts, grad, gathered)
+    )(owner, newton_counts, grad, gathered)
     theirs = lax.ppermute(theirs, REPLICA, [(i, i ^ 1) for i in range(replicas)])
 
-    payload = jnp.concatenate([coded_rows[:rows], coded_rows[rows:] + norms], axis=0)
-    words = lax.all_gather(payload, REPLICA, axis=0, tiled=False)
+    totals = totals_of(returned, rows)
+    others = lax.ppermute(totals, "refresh", [(0, 1), (1, 0)])
 
     outs = pl.pallas_call(
         finish_kernel,
         out_shape=(shape((rows, owners * order), f32),) + (shape((rows, order), f32),) * 4,
-        in_specs=[SMEM, VMEM, VMEM, VMEM],
+        in_specs=[SMEM] + [VMEM] * 5,
         out_specs=(VMEM,) * 5,
-        scratch_shapes=[pltpu.SMEM((owners,), i32)],
         name="finish",
-    )(owner, words, mine, theirs)
+    )(owner, on_chip(returned), on_chip(totals), on_chip(others), on_chip(mine), on_chip(theirs))
     return tuple(out[None] for out in outs)
 
 

time: 142 us -> 120 us (0.85)
  the two profiles are of different devices: /device:TPU:53 before, /device:TPU:2 now
where the time goes in v2:
time: 120 us
  blocking collectives  49.4 us (41%)
  starting transfers between devices  21.1 us (18%)
  Pallas kernels  19.1 us (16%)
  waiting for transfers between devices  16 us (13%)
  between operations  14.1 us (12%)
    all_to_all x1, blocking collectives, local(): arrived = lax.all_to_all(ordered, REPLICA, 0, 0, tiled=True)  26.2 us
    all_gather x1, blocking collectives, local(): words = lax.all_gather(summed, REPLICA, axis=0, tiled=False)  23.2 us
    pallas_call x1, Pallas kernels, local(): pl.pallas_call(newton_kernel, in_specs=[SMEM, SMEM, ANY, ANY], out_specs=...  10.5 us
    all_to_all x1, waiting for transfers between devices, local(): returned = lax.all_to_all(coded_blocks, MP, 0, 0, tiled=True)  10.1 us
    all_to_all x1, starting transfers between devices, local(): returned = lax.all_to_all(coded_blocks, MP, 0, 0, tiled=True)  8.33 us
    ppermute x1, starting transfers between devices, local(): summed = lax.ppermute(summed, REPLICA + MP, there)  7.82 us
    pallas_call x1, Pallas kernels, local(): pl.pallas_call(direction_kernel, out_shape=(shape((order, order), f32), s...  4.68 us
    ppermute x1, waiting for transfers between devices, local(): summed = lax.ppermute(summed, REPLICA + MP, there)  3.4 us
  transfers between devices with their start and end apart: 5, of which 3 were waited for; matrix products, arithmetic and copies ran while one was open for 0% of the time, Pallas kernels for 9%

profile of v2, /device:TPU:2, one launch (start us, length us, event | category | flops | bytes accessed | tf_op | source)
XLA Modules:
  0.0 119.7 jit_solution(10809792772355465821)
XLA Ops:
  7.2 0.0 all-gather.3.cloned.1.call-start
  7.2 1.9 %order_blocks.1 = (bf16[16,32,512]{2,1,0:T(8,128)(2,1)S(1)}, f32[32,2048]{1,0:T(8,128)}) custom-call(s32[2,16]{1,0:T(2,128)} %owner_ref.5, bf16[32,8192]{1,0:T(8,128)(2,1)} %bitcast.12, f32[32,512]{1,0:T(8,128)} %bitcast.13, f32[32,512]{1,0:T(8,128)} %bitcast.14, f32[32,512]{1,0:T(8,128)} %bitcast.15, f32[32,512]{1,0:T(8,128)} %bitcast.16), custom_call_target="tpu_custom_call" | custom-call | tf_op jit(solution)/shard_map/order_blocks/pallas_call | solution.py:292
  9.1 0.0 all-gather.3.cloned.1.call-update
  9.1 26.2 %all_to_all.10.pieces_ref = bf16[16,32,512]{2,1,0:T(8,128)(2,1)S(1)} all-to-all(bf16[16,32,512]{2,1,0:T(8,128)(2,1)S(1)} %get-tuple-element.16), channel_id=1, replica_groups=mesh['replica_0'=8,'replica_1'=2,'mp_0'=8,'mp_1'=2,'refresh'=2] {'replic..., dimensions={0} | all-to-all | bytes 1048576 | tf_op jit(solution)/shard_map/all_to_all | solution.py:301
  35.3 0.1 sum_partials.1
  35.4 7.8 %collective-permute-start = (s32[40,384]{1,0:T(8,128)S(1)}, s32[40,384]{1,0:T(8,128)S(1)}, u32[]{:S(2)}, u32[]{:S(2)}) collective-permute-start(s32[40,384]{1,0:T(8,128)S(1)} %sum_partials.1), channel_id=1, source_target_pairs={{0,16},{2,48},{4,88},{6,120},{8,128},{10,160},{12,200},{14,232},{1... | collective-permute-start | bytes 184328 | tf_op jit(solution)/shard_map/ppermute | solution.py:315
  43.2 3.4 %collective-permute-done = s32[40,384]{1,0:T(8,128)S(1)} collective-permute-done((s32[40,384]{1,0:T(8,128)S(1)}, s32[40,384]{1,0:T(8,128)S(1)}, u32[]{:S(2)}, u32[]{:S(2)}) %collective-permute-start) | collective-permute-done | bytes 61472 | tf_op jit(solution)/shard_map/ppermute | solution.py:315
  46.6 23.2 %all-gather = s32[640,384]{1,0:T(8,128)S(1)} all-gather(s32[40,384]{1,0:T(8,128)S(1)} %collective-permute-done), channel_id=2, replica_groups=mesh['replica_0'=8,'replica_1'=2,'mp_0'=8,'mp_1'=2,'refresh'=2] {'replic..., dimensions={0}, use_global_device_ids=true | all-gather | bytes 1044480 | tf_op jit(solution)/shard_map/all_gather | solution.py:316
  69.8 0.0 all-gather.3.cloned.1.call-done.inputs_ref
  69.8 4.7 %direction.1 = (f32[512,512]{1,0:T(8,128)}, s32[16,40,256]{2,1,0:T(8,128)}) custom-call(s32[16,40,384]{2,1,0:T(8,128)S(1)} %bitcast.11, f32[512,2048]{1,0:T(8,128)} %all-gather.3.cloned.1.call-done.inputs_ref), custom_call_target="tpu_custom_call" | custom-call | flops 1610612736 | bytes 5242880 | tf_op jit(solution)/shard_map/direction/pallas_call | solution.py:318
  74.5 8.3 %all-to-all-start.1 = ((s32[16,40,256]{2,1,0:T(8,128)}), s32[16,40,256]{2,1,0:T(8,128)S(1)}, u32[]{:S(2)}, u32[]{:S(2)}) async-start(s32[16,40,256]{2,1,0:T(8,128)} %get-tuple-element.18), calls=%async_computation.1 | async-start | bytes 1310720 | tf_op jit(solution)/shard_map/all_to_all | solution.py:332
  82.8 10.5 %newton.1 = (f32[64,512]{1,0:T(8,128)S(1)}, f32[64,512]{1,0:T(8,128)S(1)}) custom-call(s32[2,16]{1,0:T(2,128)} %owner_ref.5, s32[2,16]{1,0:T(2,128)} %counts_ref.1, f32[512,512]{1,0:T(8,128)} %get-tuple-element.19.grad_ref, f32[512,2048]{1,0:T(8,128)} %all-gather.3.cloned.1.call-done.inputs_ref), custom_call_target="tpu_custom_call" | custom-call | flops 12079595520 | bytes 2097152 | tf_op jit(solution)/shard_map/newton/pallas_call | solution.py:334
  93.4 2.0 %collective-permute-start.2 = (f32[64,512]{1,0:T(8,128)S(1)}, f32[64,512]{1,0:T(8,128)S(1)}, u32[]{:S(2)}, u32[]{:S(2)}) collective-permute-start(f32[64,512]{1,0:T(8,128)S(1)} %get-tuple-element.21), channel_id=1, source_target_pairs={{0,32},{32,0},{64,96},{96,64},{128,160},{160,128},{192,224},{224,1... | collective-permute-start | bytes 393224 | tf_op jit(solution)/shard_map/ppermute | solution.py:354
  95.3 10.1 %all-to-all-done.1.words_ref = s32[16,40,256]{2,1,0:T(8,128)S(1)} async-done(((s32[16,40,256]{2,1,0:T(8,128)}), s32[16,40,256]{2,1,0:T(8,128)S(1)}, u32[]{:S(2)}, u32[]{:S(2)}) %all-to-all-start.1) | async-done | bytes 655392 | tf_op jit(solution)/shard_map/all_to_all | solution.py:332
  105.5 2.9 %collective-permute-start.1 = (f32[2,128]{1,0:T(2,128)S(1)}, f32[2,128]{1,0:T(2,128)S(1)}, u32[]{:S(2)}, u32[]{:S(2)}) collective-permute-start(f32[2,128]{1,0:T(2,128)S(1)} %fusion.4.totals_ref), channel_id=1, source_target_pairs={{0,1},{1,0},{2,3},{3,2},{4,5},{5,4},{6,7},{7,6},{8,9},{9,8},{10,11... | collective-permute-start | bytes 3080 | tf_op jit(solution)/shard_map/ppermute | solution.py:357
  108.4 0.0 collective-permute-done.2.theirs_ref
  108.4 2.5 %collective-permute-done.1.others_ref = f32[2,128]{1,0:T(2,128)S(1)} collective-permute-done((f32[2,128]{1,0:T(2,128)S(1)}, f32[2,128]{1,0:T(2,128)S(1)}, u32[]{:S(2)}, u32[]{:S(2)}) %collective-permute-start.1) | collective-permute-done | bytes 1056 | tf_op jit(solution)/shard_map/ppermute | solution.py:357
  110.9 1.9 %finish.1 = (f32[32,8192]{1,0:T(8,128)}, f32[32,512]{1,0:T(8,128)}, f32[32,512]{1,0:T(8,128)}, f32[32,512]{1,0:T(8,128)}, f32[32,512]{1,0:T(8,128)}) custom-call(s32[2,16]{1,0:T(2,128)} %owner_ref.5, s32[16,40,256]{2,1,0:T(8,128)S(1)} %all-to-all-done.1.words_ref, f32[2,128]{1,0:T(2,128)S(1)} %fusion.4.totals_ref, ...), custom_call_target="tpu_custom_call" | custom-call | tf_op jit(solution)/shard_map/finish/pallas_call | solution.py:359
  (1 shorter events, 0.0 us)
Async XLA Ops:
  7.2 62.6 %all-gather.3.cloned.1.call-start = ((), (), s32[]{:S(2)}) async-start(), calls=%async_computation.2 | async-start | bytes 4456448 | tf_op jit(solution)/shard_map/all_gather | solution.py:300
  35.4 11.2 %collective-permute-start = (s32[40,384]{1,0:T(8,128)S(1)}, s32[40,384]{1,0:T(8,128)S(1)}, u32[]{:S(2)}, u32[]{:S(2)}) collective-permute-start(s32[40,384]{1,0:T(8,128)S(1)} %sum_partials.1), channel_id=1, source_target_pairs={{0,16},{2,48},{4,88},{6,120},{8,128},{10,160},{12,200},{14,232},{1... | collective-permute-start | bytes 184328 | tf_op jit(solution)/shard_map/ppermute | solution.py:315
  74.5 30.9 %all-to-all-start.1 = ((s32[16,40,256]{2,1,0:T(8,128)}), s32[16,40,256]{2,1,0:T(8,128)S(1)}, u32[]{:S(2)}, u32[]{:S(2)}) async-start(s32[16,40,256]{2,1,0:T(8,128)} %get-tuple-element.18), calls=%async_computation.1 | async-start | bytes 1310720 | tf_op jit(solution)/shard_map/all_to_all | solution.py:332
  93.4 15.0 %collective-permute-start.2 = (f32[64,512]{1,0:T(8,128)S(1)}, f32[64,512]{1,0:T(8,128)S(1)}, u32[]{:S(2)}, u32[]{:S(2)}) collective-permute-start(f32[64,512]{1,0:T(8,128)S(1)} %get-tuple-element.21), channel_id=1, source_target_pairs={{0,32},{32,0},{64,96},{96,64},{128,160},{160,128},{192,224},{224,1... | collective-permute-start | bytes 393224 | tf_op jit(solution)/shard_map/ppermute | solution.py:354
  105.5 5.5 %collective-permute-start.1 = (f32[2,128]{1,0:T(2,128)S(1)}, f32[2,128]{1,0:T(2,128)S(1)}, u32[]{:S(2)}, u32[]{:S(2)}) collective-permute-start(f32[2,128]{1,0:T(2,128)S(1)} %fusion.4.totals_ref), channel_id=1, source_target_pairs={{0,1},{1,0},{2,3},{3,2},{4,5},{5,4},{6,7},{7,6},{8,9},{9,8},{10,11... | collective-permute-start | bytes 3080 | tf_op jit(solution)/shard_map/ppermute | solution.py:357
Sparse Core Ops, SparseCore 0:
  10.7 54.4 all-gather.2
